TPU v7x, 128 devices: a whole 4x4x4 slice. The times are simulated.
128 devices in a mesh: rad: 32 (over y, z, core), ang: 4 (over x).
Axes of the slice: x: 4, y: 4, z: 4, core: 2. Of those that a mesh axis runs over, the one named last changes fastest.
Arguments:
- nonlin: bfloat16 [2, 512, 131072], P(None, 'rad', 'ang'), may hold values from -6 to 6
- state: float32 [2, 512, 131072], P(None, 'rad', 'ang'), may hold values from -6 to 6
- inverse: float32 [128, 2, 1024, 1024], P(('ang', 'rad')), may hold values from -0.1875 to 0.1875
- pair_of_slot: int32 [128], P(('ang', 'rad')), may hold values from 0 to 127, each once
Outputs:
- new_state: float32 [2, 512, 131072], P(None, 'rad', 'ang')
Inputs may be any that keep to these rules, and one draw needn't show every extreme that they name: Slot s of the window holds degrees pair_of_slot[s] and 511 - pair_of_slot[s]; every pair once.
All inputs are finite; a program needn't handle non-finite values.
Results may differ from a plain program's by a relative error of at most 0.0003.
Values may be sent and summed in bfloat16 or wider, within the bound.
A program may use at most 128 MiB of HBM per device.

v0:
```python
import math

import jax
import jax.numpy as jnp
from jax import lax
from jax.sharding import PartitionSpec as P

inner_radius = 0.35
outer_radius = 1.0
blend_weight = 0.5


def radius_at(level_index, total_levels):
    scaled = level_index / (total_levels - 1.0)
    stretch = (1.0 - blend_weight) * scaled + blend_weight * (1.0 - jnp.cos(math.pi * scaled)) / 2.0
    return inner_radius + (outer_radius - inner_radius) * stretch


def forcing(padded, old_state, total_levels):
    count = padded.shape[1] - 2
    values = padded.astype(jnp.float32)
    level_index = jnp.arange(count, dtype=jnp.float32)
    radius_here = radius_at(level_index, total_levels)
    step_below = radius_here - radius_at(level_index - 1.0, total_levels)
    step_above = radius_at(level_index + 1.0, total_levels) - radius_here
    at_inner = level_index == 0.0
    at_outer = level_index == total_levels - 1.0
    weight_below = jnp.where(
        at_inner,
        0.0,
        jnp.where(
            at_outer, -1.0 / step_below, -step_above / (step_below * (step_below + step_above))
        ),
    )
    weight_here = jnp.where(
        at_inner,
        -1.0 / step_above,
        jnp.where(
            at_outer, 1.0 / step_below, (step_above - step_below) / (step_below * step_above)
        ),
    )
    weight_above = jnp.where(
        at_inner,
        1.0 / step_above,
        jnp.where(at_outer, 0.0, step_below / (step_above * (step_below + step_above))),
    )
    centre = values[:, 1:-1]
    derivative = (
        weight_below[None, :, None] * values[:, :-2]
        + weight_here[None, :, None] * centre
        + weight_above[None, :, None] * values[:, 2:]
    )
    time_step = 0.5 * (outer_radius - inner_radius) / (total_levels - 1.0)
    return old_state + time_step * (derivative + 2.0 * centre / radius_here[None, :, None])


def lower_mask(column_count, pair_index):
    half_cols = column_count // 2
    column_index = jnp.arange(column_count, dtype=jnp.int32)
    first_half = column_index < pair_index + 1
    second_half = (column_index >= half_cols) & (column_index - half_cols < pair_index)
    return jnp.where(column_index < half_cols, first_half, second_half)


def apply_inverse(block, matrices, pair_index):
    field_count, level_count, column_count = block.shape
    row_count = field_count * level_count
    flattened = block.reshape(row_count, column_count)
    stacked = matrices.reshape(2 * row_count, row_count)
    both_parts = jnp.dot(
        stacked, flattened, precision=lax.Precision.HIGHEST, preferred_element_type=jnp.float32
    )
    both_parts = both_parts.reshape(2, row_count, column_count)
    lower_part = both_parts[0]
    upper_part = both_parts[1]
    chosen = jnp.where(lower_mask(column_count, pair_index)[None, :], lower_part, upper_part)
    return chosen.reshape(field_count, level_count, column_count)


def local(nonlin, state, inverse, pair_of_slot):
    levels = nonlin.shape[1]
    groups = lax.axis_size("rad")
    width = nonlin.shape[2] // groups
    total_levels = levels * groups * 1.0
    term_cols = lax.all_to_all(
        nonlin.reshape(2, levels, groups, width), "rad", split_axis=2, concat_axis=1, tiled=True
    )
    old_state = lax.all_to_all(
        state.reshape(2, levels, groups, width), "rad", split_axis=2, concat_axis=1, tiled=True
    )
    term_cols = term_cols.reshape(2, levels * groups, width)
    old_state = old_state.reshape(2, levels * groups, width)
    padded = jnp.pad(term_cols, ((0, 0), (1, 1), (0, 0)))
    columns = forcing(padded, old_state, total_levels)
    solved = apply_inverse(columns, inverse[0], pair_of_slot[0])
    returned = lax.all_to_all(
        solved.reshape(2, groups, levels, 1, width), "rad", split_axis=1, concat_axis=3, tiled=True
    )
    return returned.reshape(2, levels, groups * width)


def solution(mesh):
    placed = (
        P(None, "rad", "ang"),
        P(None, "rad", "ang"),
        P(("ang", "rad"), None, None, None),
        P(("ang", "rad")),
    )
    return jax.shard_map(
        local, mesh=mesh, in_specs=placed, out_specs=P(None, "rad", "ang"), check_vma=False
    )
```

profile of v0, /device:TPU:1, one launch (start us, length us, event | category | flops | bytes accessed | tf_op | source)
XLA Modules:
  0.0 245.9 jit_solution(1609782223107370576)
XLA Ops:
  0.0 3.2 %copy.26 = bf16[2,2,32,8,1024]{4,3,1,0,2:T(8,128)(2,1)} copy(bf16[2,2,32,8,1024]{4,3,2,1,0:T(8,128)(2,1)} %bitcast.45) | data formatting | bytes 4194304 | tf_op jit(solution)/shard_map/reshape | solution.py:86
  3.2 9.6 %all-to-all-start.1 = ((bf16[2,16,32,1024]{3,1,0,2:T(8,128)(2,1)}), bf16[2,16,32,1024]{3,1,0,2:T(8,128)(2,1)S(1)}, u32[]{:S(2)}, u32[]{:S(2)}) async-start(bf16[2,16,32,1024]{3,1,0,2:T(8,128)(2,1)} %bitcast.42), calls=%async_computation.1 | async-start | bytes 4194304 | tf_op jit(solution)/shard_map/all_to_all | solution.py:85
  12.8 4.8 %copy.25 = f32[2,2,32,8,1024]{4,3,1,0,2:T(8,128)} copy(f32[2,2,32,8,1024]{4,3,2,1,0:T(8,128)} %bitcast.44) | data formatting | bytes 8388608 | tf_op jit(solution)/shard_map/reshape | solution.py:89
  17.6 23.6 %all-to-all-done.1 = bf16[2,16,32,1024]{3,1,0,2:T(8,128)(2,1)S(1)} async-done(((bf16[2,16,32,1024]{3,1,0,2:T(8,128)(2,1)}), bf16[2,16,32,1024]{3,1,0,2:T(8,128)(2,1)S(1)}, u32[]{:S(2)}, u32[]{:S(2)}) %all-to-all-start.1) | async-done | bytes 2097184 | tf_op jit(solution)/shard_map/all_to_all | solution.py:85
  41.1 5.3 %all-to-all-start = ((f32[2,16,32,1024]{3,1,0,2:T(8,128)}), f32[2,16,32,1024]{3,1,0,2:T(8,128)}, u32[]{:S(2)}, u32[]{:S(2)}) async-start(f32[2,16,32,1024]{3,1,0,2:T(8,128)} %bitcast.39), calls=%async_computation | async-start | bytes 8388608 | tf_op jit(solution)/shard_map/all_to_all | solution.py:88
  47.0 0.1 fusion.14
  47.1 0.1 fusion.12
  47.2 0.2 copy.16
  47.4 2.6 %pad_convert_fusion = f32[2,514,1024]{2,1,0:T(8,128)} fusion(bf16[2,512,1024]{2,1,0:T(8,128)(2,1)S(1)} %bitcast.41), kind=kLoop, calls=%fused_computation.9 | loop fusion | flops 1052672 | bytes 6307840 | tf_op jit(solution)/shard_map/convert_element_type | solution.py:21
  50.0 48.6 %all-to-all-done = f32[2,16,32,1024]{3,1,0,2:T(8,128)} async-done(((f32[2,16,32,1024]{3,1,0,2:T(8,128)}), f32[2,16,32,1024]{3,1,0,2:T(8,128)}, u32[]{:S(2)}, u32[]{:S(2)}) %all-to-all-start) | async-done | bytes 4194336 | tf_op jit(solution)/shard_map/all_to_all | solution.py:88
  98.6 2.8 %copy.14 = f32[2,16,32,1024]{3,1,2,0:T(8,128)S(1)} copy(f32[2,16,32,1024]{3,1,0,2:T(8,128)} %all-to-all-done) | data formatting | bytes 8388608 | tf_op jit(solution)/shard_map/all_to_all | solution.py:88
  101.4 0.6 copy-done
  102.1 2.6 %fusion.3 = f32[2,512,1024]{2,1,0:T(8,128)S(1)} fusion(f32[2,514,1024]{2,1,0:T(8,128)S(1)} %copy-done, f32[2,16,32,1024]{3,1,2,0:T(8,128)S(1)} %copy.14, f32[512]{0:T(512)S(1)} %get-tuple-element.10, f32[512]{0:T(512)S(1)} %get-tuple-element.7, f32[512]{0:T(512)S(1)} %get-tuple-element.8, f32[512]{0:T(512)S(1)} %get-tuple-element.9), kind=kLoop, calls=%fused_computation.6 | loop fusion | flops 10485760 | bytes 20979712 | tf_op jit(solution)/shard_map/add | solution.py:54
  104.6 0.0 slice-done
  104.7 0.1 slice-done.1
  104.7 54.4 %convolution_bitcast_fusion = f32[2048,1024]{0,1:T(8,128)S(1)} fusion(f32[1024,1024]{1,0:T(8,128)S(1)} %bitcast.43, f32[2048,1024]{1,0:T(8,128)S(1)} %bitcast.48), kind=kOutput, calls=%fused_computation | convolution fusion | flops 25769803776 | bytes 20971520 | tf_op jit(solution)/shard_map/dot_general | solution.py:70
  159.1 4.2 %fusion.39 = (f32[1024,1024]{0,1:T(8,128)}, f32[1024,1024]{0,1:T(8,128)}) fusion(f32[2048,1024]{0,1:T(8,128)S(1)} %convolution_bitcast_fusion), kind=kLoop, calls=%fused_computation.58 | loop fusion | bytes 16777216 | tf_op jit(solution)/shard_map/slice | solution.py:75
  163.3 5.4 %copy.17 = f32[1024,1024]{1,0:T(8,128)} copy(f32[1024,1024]{0,1:T(8,128)} %get-tuple-element.6) | data formatting | bytes 8388608 | tf_op jit(solution)/shard_map/slice | solution.py:74
  168.7 5.4 %copy.18 = f32[1024,1024]{1,0:T(8,128)} copy(f32[1024,1024]{0,1:T(8,128)} %get-tuple-element.5) | data formatting | bytes 8388608 | tf_op jit(solution)/shard_map/slice | solution.py:75
  174.1 4.4 %broadcast_select_fusion = f32[2,32,16,1,1024]{4,2,1,0,3:T(8,128)S(1)} fusion(f32[2,32,16,1,1024]{4,2,1,0,3:T(8,128)} %bitcast.37, f32[2,32,16,1,1024]{4,2,1,0,3:T(8,128)} %bitcast.38, pred[1024]{0:T(1024)(128)(4,1)S(1)} %fusion.5), kind=kLoop, calls=%fused_computation.11 | loop fusion | flops 1048576 | bytes 12583936 | tf_op jit(solution)/shard_map/jit(_where)/select_n | solution.py:76
  178.5 0.6 copy.19
  179.1 57.5 %all_to_all.45 = f32[2,32,16,1,1024]{4,2,0,3,1:T(8,128)S(1)} all-to-all(f32[2,32,16,1,1024]{4,2,0,3,1:T(8,128)S(1)} %copy.19), channel_id=1, replica_groups=mesh['rad'=32,'ang'=4] {'rad'}, dimensions={1} | all-to-all | bytes 8388608 | tf_op jit(solution)/shard_map/all_to_all | solution.py:96
  236.5 4.4 %copy.20 = f32[2,1,16,32,1,1024]{5,3,2,0,4,1:T(8,128)} copy(f32[2,1,16,32,1,1024]{5,2,0,3,4,1:T(8,128)S(1)} %bitcast.40) | data formatting | bytes 8388608 | tf_op jit(solution)/shard_map/all_to_all | solution.py:96
  240.9 4.9 %reshape.130 = f32[2,16,32768]{2,1,0:T(8,128)} reshape(f32[2,1,16,32,1,1024]{5,3,2,0,4,1:T(8,128)} %copy.20) | data formatting | bytes 8388608 | tf_op jit(solution)/shard_map/reshape | solution.py:99
  (5 shorter events, 0.0 us)
Async XLA Ops:
  3.2 37.9 %all-to-all-start.1 = ((bf16[2,16,32,1024]{3,1,0,2:T(8,128)(2,1)}), bf16[2,16,32,1024]{3,1,0,2:T(8,128)(2,1)S(1)}, u32[]{:S(2)}, u32[]{:S(2)}) async-start(bf16[2,16,32,1024]{3,1,0,2:T(8,128)(2,1)} %bitcast.42), calls=%async_computation.1 | async-start | bytes 4194304 | tf_op jit(solution)/shard_map/all_to_all | solution.py:85
  41.1 57.5 %all-to-all-start = ((f32[2,16,32,1024]{3,1,0,2:T(8,128)}), f32[2,16,32,1024]{3,1,0,2:T(8,128)}, u32[]{:S(2)}, u32[]{:S(2)}) async-start(f32[2,16,32,1024]{3,1,0,2:T(8,128)} %bitcast.39), calls=%async_computation | async-start | bytes 8388608 | tf_op jit(solution)/shard_map/all_to_all | solution.py:88
  98.6 3.5 %copy-start = (f32[2,514,1024]{2,1,0:T(8,128)S(1)}, f32[2,514,1024]{2,1,0:T(8,128)}, u32[]{:S(2)}) copy-start(f32[2,514,1024]{2,1,0:T(8,128)} %pad_convert_fusion) | copy-start | bytes 12632068
  98.6 6.1 %slice-start = ((s8[8388608]{0:T(1024)(128)(4,1)}), s8[4194304]{0:T(1024)(128)(4,1)S(1)}, s32[]{:S(2)}) async-start(s8[8388608]{0:T(1024)(128)(4,1)} %bitcast.46), calls=%async_computation.3 | async-start | bytes 8388608
  102.1 2.7 %slice-start.1 = ((s8[8388608]{0:T(1024)(128)(4,1)}), s8[4194304]{0:T(1024)(128)(4,1)S(1)}, s32[]{:S(2)}) async-start(s8[8388608]{0:T(1024)(128)(4,1)} %bitcast.46), calls=%async_computation.4 | async-start | bytes 8388608
where the time goes:
time: 246 us
  waiting for transfers between devices  72.2 us (29%)
  blocking collectives  57.5 us (23%)
  matrix products  54.4 us (22%)
  local copies, waits for them, and re-layouts  36.5 us (15%)
  starting transfers between devices  14.9 us (6%)
  other arithmetic  9.72 us (4%)
    all_to_all x1, blocking collectives, local(): lax.all_to_all(solved.reshape(2, groups, levels, 1, width), 'rad', split_...  57.5 us
    dot_general x1, matrix products, apply_inverse(): jnp.dot(stacked, flattened, precision=lax.Precision.HIGHEST, preferred_el...  54.4 us
    all_to_all x1, waiting for transfers between devices, local(): lax.all_to_all(state.reshape(2, levels, groups, width), 'rad', split_axis...  48.6 us
    all_to_all x1, waiting for transfers between devices, local(): lax.all_to_all(nonlin.reshape(2, levels, groups, width), 'rad', split_axi...  23.6 us
    all_to_all x1, starting transfers between devices, local(): lax.all_to_all(nonlin.reshape(2, levels, groups, width), 'rad', split_axi...  9.59 us
    slice x2, local copies, waits for them, and re-layouts, apply_inverse(): upper_part = both_parts[1]  9.58 us
    slice x1, local copies, waits for them, and re-layouts, apply_inverse(): lower_part = both_parts[0]  5.37 us
    all_to_all x1, starting transfers between devices, local(): lax.all_to_all(state.reshape(2, levels, groups, width), 'rad', split_axis...  5.26 us
  transfers between devices with their start and end apart: 2, of which 2 were waited for; matrix products, arithmetic and copies ran while one was open for 3% of the time, Pallas kernels for 0%

commit v1 on v0

v1 whole, which is shorter than its diff:
```python
import functools
import math

import jax
import jax.numpy as jnp
import numpy as np
from jax import lax
from jax.experimental import pallas as pl
from jax.experimental.pallas import tpu as pltpu
from jax.sharding import PartitionSpec as P

inner_radius = 0.35
outer_radius = 1.0
blend_weight = 0.5

MESH = pl.DeviceIdType.MESH
LANES = 128
CHUNK_TILES = ((0, 4), (1, 2), (3, 5), (6, 7))
MIXED = 0
QMAX = 32767.0
TINY = 1e-30


def level_weights(total_levels):
    def radius_at(k):
        scaled = k / (total_levels - 1.0)
        stretch = (1.0 - blend_weight) * scaled + blend_weight * (1.0 - np.cos(math.pi * scaled)) / 2.0
        return inner_radius + (outer_radius - inner_radius) * stretch

    k = np.arange(total_levels, dtype=np.float64)
    here = radius_at(k)
    below = here - radius_at(k - 1.0)
    above = radius_at(k + 1.0) - here
    weight_below = -above / (below * (below + above))
    weight_here = (above - below) / (below * above)
    weight_above = below / (above * (below + above))
    weight_below[0], weight_here[0], weight_above[0] = 0.0, -1.0 / above[0], 1.0 / above[0]
    weight_below[-1], weight_here[-1], weight_above[-1] = -1.0 / below[-1], 1.0 / below[-1], 0.0
    dt = 0.5 * (outer_radius - inner_radius) / (total_levels - 1.0)
    return np.stack([dt * weight_below, dt * (weight_here + 2.0 / here), dt * weight_above], 0)


def step_kernel(
    groups, levels, width,
    weights_ref, nonlin_ref, state_ref, inverse_ref, pair_ref,
    outq_ref, outs_ref,
    nl, st, wt, minv, mhi, mlo, halo_f, halo_out, halo_in,
    fsrc, fdst, fss, fsd, vhi, vlo, y, bsrc, bss, outs_v,
    load_sem, inv_sem, halo_ssem, halo_rsem,
    fsend, frecv, fs_send, fs_recv, bsend, brecv, bs_send, bs_recv, out_sem,
):
    chunks = len(CHUNK_TILES)
    me = lax.axis_index("rad")
    half = groups * levels
    cw = width // chunks

    barrier = pltpu.get_barrier_semaphore()

    @pl.loop(1, groups)
    def _(j):
        pl.semaphore_signal(barrier, inc=1, device_id={"rad": lax.rem(me + j, groups)}, device_id_type=MESH)

    load_nl = pltpu.make_async_copy(nonlin_ref, nl, load_sem.at[0])
    load_st = pltpu.make_async_copy(state_ref, st, load_sem.at[1])
    load_wt = pltpu.make_async_copy(weights_ref.at[me], wt, load_sem.at[2])
    load_nl.start()
    load_wt.start()
    load_st.start()
    load_inv = [pltpu.make_async_copy(inverse_ref.at[0, m], minv.at[m], inv_sem.at[m]) for m in range(2)]
    for copy in load_inv:
        copy.start()

    load_nl.wait()

    @pl.loop(0, groups)
    def _(s):
        for f in range(2):
            for t in range(width // LANES):
                cols = pl.ds(pl.multiple_of(s * width + t * LANES, LANES), LANES)
                rows = nl[f, :, cols].astype(jnp.float32)
                at = f * (width // LANES) + t
                halo_f[0, s, at:at + 1, :] = rows[levels - 1:levels]
                halo_f[1, s, at:at + 1, :] = rows[0:1]
        for d in range(2):
            halo_out[d, s] = halo_f[d, s].astype(jnp.bfloat16)

    pl.semaphore_wait(barrier, groups - 1)
    halo_copies = []
    for d, peer in ((0, lax.rem(me + 1, groups)), (1, lax.rem(me + groups - 1, groups))):
        halo_copies.append(pltpu.make_async_remote_copy(
            src_ref=halo_out.at[d], dst_ref=halo_in.at[d], send_sem=halo_ssem.at[d], recv_sem=halo_rsem.at[d],
            device_id={"rad": peer}, device_id_type=MESH))
    for copy in halo_copies:
        copy.start()

    for m in range(2):
        load_inv[m].wait()

        @pl.loop(0, 2 * half // 64)
        def _(i, m=m):
            rows = pl.ds(pl.multiple_of(i * 64, 64), 64)
            full = minv[m, rows, :]
            high = full.astype(jnp.bfloat16)
            mhi[m, rows, :] = high
            mlo[m, rows, :] = (full - high.astype(jnp.float32)).astype(jnp.bfloat16)

    load_st.wait()
    load_wt.wait()
    for copy in halo_copies:
        copy.wait()

    def forward_copy(ch, peer):
        return pltpu.make_async_remote_copy(
            src_ref=fsrc.at[ch, peer], dst_ref=fdst.at[ch, :, me], send_sem=fsend.at[ch], recv_sem=frecv.at[ch],
            device_id={"rad": peer}, device_id_type=MESH)

    def forward_own(ch):
        return pltpu.make_async_copy(fsrc.at[ch, me], fdst.at[ch, :, me], frecv.at[ch])

    row_index = lax.broadcasted_iota(jnp.int32, (levels, LANES), 0)

    @pl.loop(0, groups)
    def _(j):
        peer = lax.rem(me + j, groups)
        col0 = pl.multiple_of(peer * width, width)
        edges = [halo_in[d, peer].astype(jnp.float32) for d in range(2)]
        tiles = {}
        largest = None
        for f in range(2):
            for t in range(width // LANES):
                cols = pl.ds(pl.multiple_of(col0 + t * LANES, LANES), LANES)
                here = nl[f, :, cols].astype(jnp.float32)
                at = f * (width // LANES) + t
                low, top = edges[0][at:at + 1], edges[1][at:at + 1]
                below = jnp.where(row_index == 0, low, pltpu.roll(here, 1, 0))
                above = jnp.where(row_index == levels - 1, top, pltpu.roll(here, levels - 1, 0))
                value = st[f, :, cols] + (wt[0] * below + wt[1] * here + wt[2] * above)
                tiles[f, t] = value
                size = jnp.abs(value)
                largest = size if largest is None else jnp.maximum(largest, size)
        largest = jnp.maximum(jnp.max(largest, axis=0, keepdims=True), TINY)
        fss[peer] = largest * (1.0 / QMAX)
        factor = QMAX / largest
        for ch, members in enumerate(CHUNK_TILES):
            for n, t in enumerate(members):
                for f in range(2):
                    code = jnp.round(tiles[f, t] * factor).astype(jnp.int32).astype(jnp.int16)
                    fsrc[ch, peer, f, :, n * LANES:(n + 1) * LANES] = code

        @pl.when(j > 0)
        def _():
            pltpu.make_async_remote_copy(
                src_ref=fss.at[peer], dst_ref=fsd.at[me], send_sem=fs_send, recv_sem=fs_recv,
                device_id={"rad": peer}, device_id_type=MESH).start()
            forward_copy(0, peer).start()

        @pl.when(j == 0)
        def _():
            pltpu.make_async_copy(fss.at[me], fsd.at[me], fs_recv).start()
            forward_own(0).start()

    for ch in range(1, chunks):
        forward_own(ch).start()

        @pl.loop(1, groups)
        def _(j, ch=ch):
            forward_copy(ch, lax.rem(me + j, groups)).start()

    pair = pair_ref[0]
    pltpu.make_async_copy(fsd, fsd, fs_recv).wait()
    for ch, members in enumerate(CHUNK_TILES):
        pltpu.make_async_copy(fdst.at[ch], fdst.at[ch], frecv.at[ch]).wait()

        @pl.loop(0, groups)
        def _(r, ch=ch):
            scale = jnp.concatenate([fsd[r]] * (cw // LANES), axis=1)
            for f in range(2):
                value = fdst[ch, f, r].astype(jnp.int32).astype(jnp.float32) * scale
                high = value.astype(jnp.bfloat16)
                rows = pl.ds(pl.multiple_of(f * half + r * levels, levels), levels)
                vhi[rows, :] = high
                vlo[rows, :] = (value - high.astype(jnp.float32)).astype(jnp.bfloat16)

        @pl.loop(0, 2 * half // 256)
        def _(i, ch=ch, members=members):
            rows = pl.ds(pl.multiple_of(i * 256, 256), 256)

            def product(m):
                dot = functools.partial(jnp.dot, preferred_element_type=jnp.float32)
                return (dot(mhi[m, rows, :], vhi[...]) + dot(mhi[m, rows, :], vlo[...])) + dot(mlo[m, rows, :], vhi[...])

            upper = product(1)
            if ch == MIXED:
                lower = product(0)
                lane = lax.broadcasted_iota(jnp.int32, (256, cw), 1)
                order = jnp.where(lane < LANES, lane, lane - LANES + 1)
                y[rows, :] = jnp.where(order < pair + 1, lower, upper)
            else:
                y[rows, :] = upper

        @pl.loop(0, groups)
        def _(j, ch=ch):
            peer = lax.rem(me + j, groups)
            values = [
                y[pl.ds(pl.multiple_of(f * half + peer * levels, levels), levels), n * LANES:(n + 1) * LANES]
                for f in range(2) for n in range(cw // LANES)
            ]
            largest = functools.reduce(jnp.maximum, [jnp.abs(value) for value in values])
            largest = jnp.maximum(jnp.max(largest, axis=0, keepdims=True), TINY)
            bss[ch, peer] = largest * (1.0 / QMAX)
            factor = QMAX / largest
            for f in range(2):
                for n in range(cw // LANES):
                    value = values[f * (cw // LANES) + n]
                    code = jnp.round(value * factor).astype(jnp.int32).astype(jnp.int16)
                    bsrc[ch, peer, f, :, n * LANES:(n + 1) * LANES] = code

            @pl.when(j > 0)
            def _():
                pltpu.make_async_remote_copy(
                    src_ref=bss.at[ch, peer], dst_ref=outs_v.at[ch, me], send_sem=bs_send.at[ch],
                    recv_sem=bs_recv.at[ch], device_id={"rad": peer}, device_id_type=MESH).start()
                pltpu.make_async_remote_copy(
                    src_ref=bsrc.at[ch, peer], dst_ref=outq_ref.at[ch, me], send_sem=bsend.at[ch],
                    recv_sem=brecv.at[ch], device_id={"rad": peer}, device_id_type=MESH).start()

            @pl.when(j == 0)
            def _():
                pltpu.make_async_copy(bss.at[ch, me], outs_v.at[ch, me], bs_recv.at[ch]).start()
                pltpu.make_async_copy(bsrc.at[ch, me], outq_ref.at[ch, me], brecv.at[ch]).start()

    others = pl.ds(0, groups - 1)
    for ch in range(chunks):
        pltpu.make_async_copy(outs_v.at[ch], outs_v.at[ch], bs_recv.at[ch]).wait()
    store = pltpu.make_async_copy(outs_v, outs_ref, out_sem)
    store.start()
    pltpu.make_async_copy(fss.at[others], fss.at[others], fs_send).wait()
    for ch in range(chunks):
        pltpu.make_async_copy(fsrc.at[ch, others], fsrc.at[ch, others], fsend.at[ch]).wait()
        pltpu.make_async_copy(bsrc.at[ch, others], bsrc.at[ch, others], bsend.at[ch]).wait()
        pltpu.make_async_copy(bss.at[ch, others], bss.at[ch, others], bs_send.at[ch]).wait()
        pltpu.make_async_copy(outq_ref.at[ch], outq_ref.at[ch], brecv.at[ch]).wait()
    store.wait()


def decode_kernel(slots, width, q_ref, s_ref, o_ref):
    for s in range(slots):
        for ch, members in enumerate(CHUNK_TILES):
            scale = s_ref[ch, s]
            for n, t in enumerate(members):
                for f in range(2):
                    code = q_ref[ch, s, f, :, n * LANES:(n + 1) * LANES]
                    o_ref[f, :, s * width + t * LANES:s * width + (t + 1) * LANES] = (
                        code.astype(jnp.int32).astype(jnp.float32) * scale
                    )


def local(nonlin, state, inverse, pair_of_slot):
    levels = nonlin.shape[1]
    groups = lax.axis_size("rad")
    width = nonlin.shape[2] // groups
    total = levels * groups
    chunks = len(CHUNK_TILES)
    cw = width // chunks
    weights = level_weights(total).reshape(3, groups, levels).transpose(1, 0, 2)[..., None]
    weights = jnp.asarray(np.broadcast_to(weights, (groups, 3, levels, LANES)).astype(np.float32))
    anywhere = pl.BlockSpec(memory_space=pl.ANY)
    q_shape = (chunks, groups, 2, levels, cw)
    s_shape = (chunks, groups, 1, LANES)
    dma = pltpu.SemaphoreType.DMA
    outq, outs = pl.pallas_call(
        functools.partial(step_kernel, groups, levels, width),
        out_shape=(jax.ShapeDtypeStruct(q_shape, jnp.int16), jax.ShapeDtypeStruct(s_shape, jnp.float32)),
        in_specs=[anywhere] * 4 + [pl.BlockSpec(memory_space=pltpu.SMEM)],
        out_specs=(anywhere, anywhere),
        scratch_shapes=[
            pltpu.VMEM(nonlin.shape, jnp.bfloat16),
            pltpu.VMEM(state.shape, jnp.float32),
            pltpu.VMEM((3, levels, LANES), jnp.float32),
            pltpu.VMEM((2, 2 * total, 2 * total), jnp.float32),
            pltpu.VMEM((2, 2 * total, 2 * total), jnp.bfloat16),
            pltpu.VMEM((2, 2 * total, 2 * total), jnp.bfloat16),
            pltpu.VMEM((2, groups, 2 * width // LANES, LANES), jnp.float32),
            pltpu.VMEM((2, groups, 2 * width // LANES, LANES), jnp.bfloat16),
            pltpu.VMEM((2, groups, 2 * width // LANES, LANES), jnp.bfloat16),
            pltpu.VMEM(q_shape, jnp.int16),
            pltpu.VMEM((chunks, 2, groups, levels, cw), jnp.int16),
            pltpu.VMEM((groups, 1, LANES), jnp.float32),
            pltpu.VMEM((groups, 1, LANES), jnp.float32),
            pltpu.VMEM((2 * total, cw), jnp.bfloat16),
            pltpu.VMEM((2 * total, cw), jnp.bfloat16),
            pltpu.VMEM((2 * total, cw), jnp.float32),
            pltpu.VMEM(q_shape, jnp.int16),
            pltpu.VMEM(s_shape, jnp.float32),
            pltpu.VMEM(s_shape, jnp.float32),
            dma((3,)), dma((2,)), dma((2,)), dma((2,)),
            dma((chunks,)), dma((chunks,)), dma, dma,
            dma((chunks,)), dma((chunks,)), dma((chunks,)), dma((chunks,)), dma,
        ],
        compiler_params=pltpu.CompilerParams(
            collective_id=0, has_side_effects=True, vmem_limit_bytes=56 * 2**20),
        name="radial_step",
    )(weights, nonlin, state, inverse, pair_of_slot)

    slots = 4
    return pl.pallas_call(
        functools.partial(decode_kernel, slots, width),
        out_shape=jax.ShapeDtypeStruct(state.shape, jnp.float32),
        grid=(groups // slots,),
        in_specs=[
            pl.BlockSpec((chunks, slots, 2, levels, cw), lambda i: (0, i, 0, 0, 0)),
            pl.BlockSpec((chunks, slots, 1, LANES), lambda i: (0, i, 0, 0)),
        ],
        out_specs=pl.BlockSpec((2, levels, slots * width), lambda i: (0, 0, i)),
        name="decode",
    )(outq, outs)


def solution(mesh):
    placed = (
        P(None, "rad", "ang"),
        P(None, "rad", "ang"),
        P(("ang", "rad"), None, None, None),
        P(("ang", "rad")),
    )
    return jax.shard_map(
        local, mesh=mesh, in_specs=placed, out_specs=P(None, "rad", "ang"), check_vma=False
    )
```

time: 246 us -> 70.6 us (0.29)
  waiting for transfers between devices: 72.2 us -> 0 us
  Pallas kernels: 0 us -> 69.7 us
  blocking collectives: 57.5 us -> 0 us
  matrix products: 54.4 us -> 0 us
  local copies, waits for them, and re-layouts: 36.5 us -> 0 us
  starting transfers between devices: 14.9 us -> 0 us
  other arithmetic: 9.72 us -> 0 us
    all_to_all x2 -> x0, waiting for transfers between devices: 72.2 us -> none  [the longest x1 48.6 us: local(): lax.all_to_all(state.reshape(2, levels, groups, width), 'rad', split_axis...]
    pallas_call x0 -> x2, Pallas kernels: none -> 69.7 us  [the longest x1 63.6 us: local(): pl.pallas_call(functools.partial(step_kernel, groups, levels, width), out...]
    all_to_all x1 -> x0, blocking collectives: 57.5 us -> none  [local(): lax.all_to_all(solved.reshape(2, groups, levels, 1, width), 'rad', split_...]
    dot_general x1 -> x0, matrix products: 54.4 us -> none  [apply_inverse(): jnp.dot(stacked, flattened, precision=lax.Precision.HIGHEST, preferred_el...]
    slice x3 -> x0, local copies, waits for them, and re-layouts: 14.9 us -> none  [the longest x2 9.58 us: apply_inverse(): upper_part = both_parts[1]]
    all_to_all x2 -> x0, starting transfers between devices: 14.9 us -> none  [the longest x1 9.59 us: local(): lax.all_to_all(nonlin.reshape(2, levels, groups, width), 'rad', split_axi...]
    reshape x3 -> x0, local copies, waits for them, and re-layouts: 12.9 us -> none  [the longest x1 4.94 us: local(): return returned.reshape(2, levels, groups * width)]
    all_to_all x3 -> x0, local copies, waits for them, and re-layouts: 7.41 us -> none  [the longest x1 4.39 us: local(): lax.all_to_all(solved.reshape(2, groups, levels, 1, width), 'rad', split_...]
  transfers between devices with their start and end apart: 2 -> 0, of which waited for: 2 -> 0; matrix products, arithmetic and copies ran while one was open for 3% -> 0% of each run, Pallas kernels for 0% -> 0%
where the time goes in v1:
time: 70.6 us; the launch traced here: 70.3 us
  Pallas kernels  69.7 us (99%)
    pallas_call x1, Pallas kernels, local(): pl.pallas_call(functools.partial(step_kernel, groups, levels, width), out...  63.6 us
    pallas_call x1, Pallas kernels, local(): pl.pallas_call(functools.partial(decode_kernel, slots, width), out_shape=...  6.07 us

profile of v1, /device:TPU:1, one launch (start us, length us, event | category | flops | bytes accessed | tf_op | source)
XLA Modules:
  0.0 70.3 jit_solution(12065600950996885827)
XLA Ops:
  0.7 63.6 %radial_step.1 = (s16[4,32,2,16,256]{4,3,2,1,0:T(8,128)(2,1)}, f32[4,32,1,128]{3,2,1,0:T(1,128)}) custom-call(f32[32,3,16,128]{3,2,1,0:T(8,128)} %constant.2.clone.weights_ref, bf16[2,16,32768]{2,1,0:T(8,128)(2,1)} %nonlin_ref.1, f32[2,16,32768]{2,1,0:T(8,128)} %state_ref.1, f32[1,2,1024,1024]{3,2,1,0:T(8,128)} %inverse_ref.1, s32[1]{0:T(128)S(6)} %copy.6.pair_ref), custom_call_target="tpu_custom_call" | custom-call | tf_op jit(solution)/shard_map/radial_step/pallas_call | solution.py:271
  64.3 6.1 %decode.1 = f32[2,16,32768]{2,1,0:T(8,128)} custom-call(s16[4,32,2,16,256]{4,3,2,1,0:T(8,128)(2,1)} %get-tuple-element.7.q_ref, f32[4,32,1,128]{3,2,1,0:T(1,128)} %get-tuple-element.8.s_ref), custom_call_target="tpu_custom_call" | custom-call | tf_op jit(solution)/shard_map/decode/pallas_call | solution.py:306

commit v2 on v1

--- a/solution.py
+++ b/solution.py
@@ -19,6 +19,25 @@
 MIXED = 0
 QMAX = 32767.0
 TINY = 1e-30
+ORDER = (
+    8, 24, 2, 20, 6, 12, 28, 10, 30, 4, 16, 14, 26, 18, 22, 9,
+    25, 3, 21, 7, 13, 29, 11, 31, 5, 17, 15, 27, 19, 23, 1,
+)
+
+
+def offset_words(order):
+    padded = [0] + list(order)
+    return [sum(d << (5 * n) for n, d in enumerate(padded[i:i + 4])) for i in range(0, len(padded), 4)]
+
+
+def peer_at(me, j):
+    word = functools.reduce(
+        lambda rest, n: jnp.where(j // 4 == n, WORDS[n], rest), range(1, len(WORDS)), WORDS[0])
+    step = (word >> (5 * lax.rem(j, 4))) & 31
+    return ((me + (step & 24)) & 24) | ((me + (step & 6)) & 6) | ((me ^ step) & 1)
+
+
+WORDS = offset_words(ORDER)
 
 
 def level_weights(total_levels):
@@ -93,17 +112,6 @@
     for copy in halo_copies:
         copy.start()
 
-    for m in range(2):
-        load_inv[m].wait()
-
-        @pl.loop(0, 2 * half // 64)
-        def _(i, m=m):
-            rows = pl.ds(pl.multiple_of(i * 64, 64), 64)
-            full = minv[m, rows, :]
-            high = full.astype(jnp.bfloat16)
-            mhi[m, rows, :] = high
-            mlo[m, rows, :] = (full - high.astype(jnp.float32)).astype(jnp.bfloat16)
-
     load_st.wait()
     load_wt.wait()
     for copy in halo_copies:
@@ -121,7 +129,7 @@
 
     @pl.loop(0, groups)
     def _(j):
-        peer = lax.rem(me + j, groups)
+        peer = peer_at(me, j)
         col0 = pl.multiple_of(peer * width, width)
         edges = [halo_in[d, peer].astype(jnp.float32) for d in range(2)]
         tiles = {}
@@ -164,7 +172,18 @@
 
         @pl.loop(1, groups)
         def _(j, ch=ch):
-            forward_copy(ch, lax.rem(me + j, groups)).start()
+            forward_copy(ch, peer_at(me, j)).start()
+
+    for m in range(2):
+        load_inv[m].wait()
+
+        @pl.loop(0, 2 * half // 64)
+        def _(i, m=m):
+            rows = pl.ds(pl.multiple_of(i * 64, 64), 64)
+            full = minv[m, rows, :]
+            high = full.astype(jnp.bfloat16)
+            mhi[m, rows, :] = high
+            mlo[m, rows, :] = (full - high.astype(jnp.float32)).astype(jnp.bfloat16)
 
     pair = pair_ref[0]
     pltpu.make_async_copy(fsd, fsd, fs_recv).wait()
@@ -200,7 +219,7 @@
 
         @pl.loop(0, groups)
         def _(j, ch=ch):
-            peer = lax.rem(me + j, groups)
+            peer = peer_at(me, j)
             values = [
                 y[pl.ds(pl.multiple_of(f * half + peer * levels, levels), levels), n * LANES:(n + 1) * LANES]
                 for f in range(2) for n in range(cw // LANES)
@@ -243,16 +262,39 @@
     store.wait()
 
 
-def decode_kernel(slots, width, q_ref, s_ref, o_ref):
-    for s in range(slots):
-        for ch, members in enumerate(CHUNK_TILES):
-            scale = s_ref[ch, s]
-            for n, t in enumerate(members):
-                for f in range(2):
-                    code = q_ref[ch, s, f, :, n * LANES:(n + 1) * LANES]
-                    o_ref[f, :, s * width + t * LANES:s * width + (t + 1) * LANES] = (
-                        code.astype(jnp.int32).astype(jnp.float32) * scale
-                    )
+def decode_kernel(parts, groups, width, q_ref, s_ref, o_ref, q, s, o, s_sem, in_sem, out_sem):
+    each = groups // parts
+    scales = pltpu.make_async_copy(s_ref, s, s_sem)
+    scales.start()
+
+    def load(i):
+        slots = pl.ds(i * each, each)
+        return pltpu.make_async_copy(q_ref.at[:, slots], q.at[:, slots], in_sem.at[i])
+
+    def store(i):
+        cols = pl.ds(pl.multiple_of(i * each * width, each * width), each * width)
+        return pltpu.make_async_copy(o.at[:, :, cols], o_ref.at[:, :, cols], out_sem.at[i])
+
+    for i in range(parts):
+        load(i).start()
+    scales.wait()
+
+    @pl.loop(0, parts)
+    def _(i):
+        load(i).wait()
+        for k in range(each):
+            slot = i * each + k
+            for ch, members in enumerate(CHUNK_TILES):
+                scale = s[ch, slot]
+                for n, t in enumerate(members):
+                    cols = pl.ds(pl.multiple_of(slot * width + t * LANES, LANES), LANES)
+                    for f in range(2):
+                        code = q[ch, slot, f, :, n * LANES:(n + 1) * LANES]
+                        o[f, :, cols] = code.astype(jnp.int32).astype(jnp.float32) * scale
+        store(i).start()
+
+    for i in range(parts):
+        store(i).wait()
 
 
 def local(nonlin, state, inverse, pair_of_slot):
@@ -302,16 +344,18 @@
         name="radial_step",
     )(weights, nonlin, state, inverse, pair_of_slot)
 
-    slots = 4
+    parts = 8
     return pl.pallas_call(
-        functools.partial(decode_kernel, slots, width),
+        functools.partial(decode_kernel, parts, groups, width),
         out_shape=jax.ShapeDtypeStruct(state.shape, jnp.float32),
-        grid=(groups // slots,),
-        in_specs=[
-            pl.BlockSpec((chunks, slots, 2, levels, cw), lambda i: (0, i, 0, 0, 0)),
-            pl.BlockSpec((chunks, slots, 1, LANES), lambda i: (0, i, 0, 0)),
+        in_specs=[anywhere] * 2,
+        out_specs=anywhere,
+        scratch_shapes=[
+            pltpu.VMEM(q_shape, jnp.int16),
+            pltpu.VMEM(s_shape, jnp.float32),
+            pltpu.VMEM(state.shape, jnp.float32),
+            dma, dma((parts,)), dma((parts,)),
         ],
-        out_specs=pl.BlockSpec((2, levels, slots * width), lambda i: (0, 0, i)),
         name="decode",
     )(outq, outs)
 

time: 70.6 us -> 66.1 us (0.936)
  Pallas kernels: 69.7 us -> 65.3 us
    pallas_call x1, Pallas kernels: 6.07 us -> 3.62 us  [local(): pl.pallas_call(functools.partial(decode_kernel, parts, groups, width), ou...]
    pallas_call x1, Pallas kernels: 63.6 us -> 61.7 us  [local(): pl.pallas_call(functools.partial(step_kernel, groups, levels, width), out...]
where the time goes in v2:
time: 66.1 us; the launch traced here: 66 us
  Pallas kernels  65.3 us (99%)
    pallas_call x1, Pallas kernels, local(): pl.pallas_call(functools.partial(step_kernel, groups, levels, width), out...  61.7 us
    pallas_call x1, Pallas kernels, local(): pl.pallas_call(functools.partial(decode_kernel, parts, groups, width), ou...  3.62 us

profile of v2, /device:TPU:1, one launch (start us, length us, event | category | flops | bytes accessed | tf_op | source)
XLA Modules:
  0.0 66.0 jit_solution(7938862653483731804)
XLA Ops:
  0.7 61.7 %radial_step.1 = (s16[4,32,2,16,256]{4,3,2,1,0:T(8,128)(2,1)}, f32[4,32,1,128]{3,2,1,0:T(1,128)}) custom-call(f32[32,3,16,128]{3,2,1,0:T(8,128)} %constant.2.clone.weights_ref, bf16[2,16,32768]{2,1,0:T(8,128)(2,1)} %nonlin_ref.1, f32[2,16,32768]{2,1,0:T(8,128)} %state_ref.1, f32[1,2,1024,1024]{3,2,1,0:T(8,128)} %inverse_ref.1, s32[1]{0:T(128)S(6)} %copy.6.pair_ref), custom_call_target="tpu_custom_call" | custom-call | tf_op jit(solution)/shard_map/radial_step/pallas_call | solution.py:313
  62.4 3.6 %decode.1 = f32[2,16,32768]{2,1,0:T(8,128)} custom-call(s16[4,32,2,16,256]{4,3,2,1,0:T(8,128)(2,1)} %get-tuple-element.7.q_ref, f32[4,32,1,128]{3,2,1,0:T(1,128)} %get-tuple-element.8.s_ref), custom_call_target="tpu_custom_call" | custom-call | tf_op jit(solution)/shard_map/decode/pallas_call | solution.py:348
